TPU v7x, 32 devices: a whole 2x2x4 slice. The times are simulated.
32 devices in a mesh: seq: 8 (over z, y), batch: 4 (over x, core).
Axes of the slice: x: 2, y: 2, z: 4, core: 2. Of those that a mesh axis runs over, the one named last changes fastest.
Arguments:
- tokens: bfloat16 [4, 8192, 1024], P('batch', 'seq'), may hold values from -6 to 6
- logits: bfloat16 [4, 8192, 256], P('batch', 'seq'), may hold values from -160 to 160
- slot_grad: bfloat16 [4, 256, 1024], P('batch', 'seq'), may hold values from -6 to 6
- phi_param: bfloat16 [1024, 256], P('seq'), may hold values from -0.1875 to 0.1875
Outputs:
- token_grad: bfloat16 [4, 8192, 1024], P('batch', 'seq')
- phi_grad: float32 [1024, 256], P('seq')
All inputs are finite; a program needn't handle non-finite values.
Results may differ from a plain program's by a relative error of at most 0.0049.
Values may be sent and summed in bfloat16 or wider, within the bound.
A program may use at most 64 MiB of HBM per device.

v0:
```python
import jax
import jax.numpy as jnp
from jax import lax
from jax.sharding import PartitionSpec as P


def per_device(tokens, logits, slot_grad, phi_param):
    inputs = tokens[0]
    scores = logits[0].astype(jnp.float32)
    upstream, phi_full = (
        lax.all_gather(slot_grad[0], "seq", axis=0, tiled=True),
        lax.all_gather(phi_param, "seq", axis=0, tiled=True),
    )
    weight_grad = lax.dot_general(
        inputs, upstream, (((1,), (1,)), ((), ())), preferred_element_type=jnp.float32
    )
    col_peak = lax.pmax(jnp.max(scores, axis=0, keepdims=True), "seq")
    raw_weights = jnp.exp(scores - col_peak)
    col_total = lax.psum(jnp.sum(raw_weights, axis=0, keepdims=True), "seq")
    dispatch = raw_weights / col_total
    col_dot = lax.psum(jnp.sum(dispatch * weight_grad, axis=0, keepdims=True), "seq")
    logit_grad = (dispatch * (weight_grad - col_dot)).astype(jnp.bfloat16)
    dispatch_low = dispatch.astype(jnp.bfloat16)
    grad_scale = float(lax.axis_size("seq") * inputs.shape[0] // 16)
    token_sum = jnp.dot(dispatch_low, upstream, preferred_element_type=jnp.float32)
    token_sum = token_sum + lax.dot_general(
        logit_grad, phi_full, (((1,), (1,)), ((), ())), preferred_element_type=jnp.float32
    )
    token_grad = (grad_scale * token_sum).astype(jnp.bfloat16)[None]
    phi_terms = lax.dot_general(
        inputs, logit_grad, (((0,), (0,)), ((), ())), preferred_element_type=jnp.float32
    )
    phi_share = lax.psum_scatter(phi_terms, "seq", scatter_dimension=0, tiled=True)
    phi_grad = lax.psum(phi_share, "batch")
    return (token_grad, phi_grad)


def solution(mesh):
    return jax.shard_map(
        per_device,
        mesh=mesh,
        in_specs=(
            P("batch", "seq", None),
            P("batch", "seq", None),
            P("batch", "seq", None),
            P("seq", None),
        ),
        out_specs=(P("batch", "seq", None), P("seq", None)),
        check_vma=False,
    )
```

profile of v0, /device:TPU:0, one launch (start us, length us, event | category | flops | bytes accessed | tf_op | source)
XLA Modules:
  0.0 210.9 jit_solution(2274995212261977552)
XLA Ops:
  7.2 0.0 copy-start
  7.2 0.0 reduce-scatter.2.cloned.1.call-start
  7.2 1.3 reduce_max.16
  8.6 23.2 %pmax.7 = f32[256]{0:T(256)S(1)} all-reduce(bf16[256]{0:T(256)(128)(2,1)S(1)} %reduce_max.16), channel_id=1, replica_groups=mesh['seq'=8,'batch'=4] {'seq'}, use_global_device_ids=true, to_apply=%region_1.0 | all-reduce | flops 256 | bytes 1536 | tf_op jit(solution)/shard_map/pmax | solution.py:17
  31.7 1.3 fusion.10
  33.0 17.1 %psum.21 = f32[256]{0:T(256)S(1)} all-reduce(f32[256]{0:T(256)S(1)} %fusion.10), channel_id=1, replica_groups=mesh['seq'=8,'batch'=4] {'seq'}, use_global_device_ids=true, to_apply=%region_3.0 | all-reduce | flops 256 | bytes 2048 | tf_op jit(solution)/shard_map/psum | solution.py:19
  50.1 31.5 %all-gather = bf16[1,256,1024]{2,1,0:T(8,128)(2,1)S(1)} all-gather(bf16[1,32,1024]{2,1,0:T(8,128)(2,1)} %param.6), channel_id=2, replica_groups=mesh['seq'=8,'batch'=4] {'seq'}, dimensions={1}, use_global_device_ids=true | all-gather | bytes 589824 | tf_op jit(solution)/shard_map/all_gather | solution.py:11
  81.6 0.0 copy-done
  81.6 0.0 copy-start.2
  81.6 0.0 copy-start.1
  81.6 3.0 %multiply_reduce_fusion = (f32[256]{0:T(256)S(1)}, f32[1024,256]{1,0:T(8,128)}) fusion(f32[256]{0:T(256)S(1)} %psum.21, f32[256]{0:T(256)S(1)} %pmax.7, bf16[1,1024,256]{2,1,0:T(8,128)(2,1)} %param.5, bf16[1,256,1024]{2,1,0:T(8,128)(2,1)S(1)} %all-gather, bf16[1,1024,1024]{2,1,0:T(8,128)(2,1)S(1)} %copy-done), kind=kOutput, calls=%fused_computation.12 | convolution fusion | flops 538181376 | bytes 4197376 | tf_op jit(solution)/shard_map/dot_general | solution.py:14
  84.6 0.0 copy-done.2
  84.6 19.4 %psum.22 = f32[256]{0:T(256)S(1)} all-reduce(f32[256]{0:T(256)S(1)} %get-tuple-element.4), channel_id=1, replica_groups=mesh['seq'=8,'batch'=4] {'seq'}, use_global_device_ids=true, to_apply=%region_5.0 | all-reduce | flops 256 | bytes 2048 | tf_op jit(solution)/shard_map/psum | solution.py:21
  103.9 0.0 copy-done.1
  103.9 0.0 copy-start.3
  103.9 3.0 %fusion.5 = f32[1024,256]{0,1:T(8,128)} fusion(bf16[1,1024,1024]{2,1,0:T(8,128)(2,1)S(1)} %copy-done, f32[1024,256]{1,0:T(8,128)} %get-tuple-element.5, f32[256]{0:T(256)S(1)} %psum.22, f32[256]{0:T(256)S(1)} %psum.21, f32[256]{0:T(256)S(1)} %pmax.7, bf16[1,1024,256]{2,1,0:T(8,128)(2,1)S(1)} %copy-done.1), kind=kOutput, calls=%fused_computation.6 | convolution fusion | flops 538443776 | bytes 4721664 | tf_op jit(solution)/shard_map/dot_general | solution.py:30
  107.0 0.0 reduce-scatter.2.cloned.1.call-update
  107.0 0.0 all-reduce.2.cloned.1.call-start
  107.0 0.0 copy-done.3
  107.0 31.8 %all_gather.7 = bf16[1024,256]{1,0:T(8,128)(2,1)S(1)} all-gather(bf16[128,256]{1,0:T(8,128)(2,1)S(1)} %copy-done.3), channel_id=1, replica_groups=mesh['seq'=8,'batch'=4] {'seq'}, dimensions={0}, use_global_device_ids=true | all-gather | bytes 589824 | tf_op jit(solution)/shard_map/all_gather | solution.py:12
  138.8 3.7 %fusion.12 = f32[1024,1024]{1,0:T(8,128)} fusion(bf16[1,256,1024]{2,1,0:T(8,128)(2,1)} %copy-done.2, bf16[1,1024,256]{2,1,0:T(8,128)(2,1)S(1)} %copy-done.1, f32[256]{0:T(256)S(1)} %psum.21, f32[256]{0:T(256)S(1)} %pmax.7), kind=kOutput, calls=%fused_computation.14 | convolution fusion | flops 537919488 | bytes 5244928 | tf_op jit(solution)/shard_map/dot_general | solution.py:25
  142.5 26.9 %reduce-scatter.2.cloned.1.call-done = f32[128,256]{0,1:T(8,128)} async-done(((f32[1024,256]{0,1:T(8,128)}), f32[128,256]{0,1:T(8,128)}) %reduce-scatter.2.cloned.1.call-update) | async-done | bytes 131088 | tf_op jit(solution)/shard_map/reduce_scatter | solution.py:33
  169.4 0.0 all-reduce.2.cloned.1.call-update
  169.4 4.7 %fusion.4 = bf16[1,1024,1024]{2,1,0:T(8,128)(2,1)} fusion(f32[1024,1024]{1,0:T(8,128)} %fusion.12, bf16[1024,256]{1,0:T(8,128)(2,1)S(1)} %all_gather.7, f32[1024,256]{1,0:T(8,128)} %get-tuple-element.5, f32[256]{0:T(256)S(1)} %psum.22, f32[256]{0:T(256)S(1)} %psum.21, f32[256]{0:T(256)S(1)} %pmax.7, bf16[1,1024,256]{2,1,0:T(8,128)(2,1)S(1)} %copy-done.1), kind=kOutput, calls=%fused_computation.5 | convolution fusion | flops 541589504 | bytes 8391680 | tf_op jit(solution)/shard_map/dot_general | solution.py:26
  174.1 28.3 %all-reduce.2.cloned.1.call-done = f32[128,256]{0,1:T(8,128)} async-done(((f32[128,256]{0,1:T(8,128)}), f32[128,256]{0,1:T(8,128)}) %all-reduce.2.cloned.1.call-update) | async-done | bytes 131088 | tf_op jit(solution)/shard_map/psum | solution.py:34
  202.4 1.7 copy.6
Async XLA Ops:
  7.2 74.4 %copy-start = (bf16[1,1024,1024]{2,1,0:T(8,128)(2,1)S(1)}, bf16[1,1024,1024]{2,1,0:T(8,128)(2,1)}, u32[]{:S(2)}) copy-start(bf16[1,1024,1024]{2,1,0:T(8,128)(2,1)} %param.4) | copy-start | bytes 6291460
  7.2 162.2 %reduce-scatter.2.cloned.1.call-start = ((), (), s32[]{:S(2)}) async-start(), calls=%async_computation.1 | async-start | bytes 1179648 | tf_op jit(solution)/shard_map/reduce_scatter | solution.py:33
  81.6 3.0 %copy-start.2 = (bf16[1,256,1024]{2,1,0:T(8,128)(2,1)}, bf16[1,256,1024]{2,1,0:T(8,128)(2,1)S(1)}, u32[]{:S(2)}) copy-start(bf16[1,256,1024]{2,1,0:T(8,128)(2,1)S(1)} %all-gather) | copy-start | bytes 1572868
  81.6 22.3 %copy-start.1 = (bf16[1,1024,256]{2,1,0:T(8,128)(2,1)S(1)}, bf16[1,1024,256]{2,1,0:T(8,128)(2,1)}, u32[]{:S(2)}) copy-start(bf16[1,1024,256]{2,1,0:T(8,128)(2,1)} %param.5) | copy-start | bytes 1572868
  103.9 3.1 %copy-start.3 = (bf16[128,256]{1,0:T(8,128)(2,1)S(1)}, bf16[128,256]{1,0:T(8,128)(2,1)}, u32[]{:S(2)}) copy-start(bf16[128,256]{1,0:T(8,128)(2,1)} %param.7) | copy-start | bytes 196612
  107.0 95.4 %all-reduce.2.cloned.1.call-start = ((), (), s32[]{:S(2)}) async-start(), calls=%async_computation.2 | async-start | bytes 262144 | tf_op jit(solution)/shard_map/psum | solution.py:34
Sparse Core Ops, SparseCore 0:
  107.1 62.2 reduce-scatter.1
  171.7 30.6 all-reduce.1
where the time goes:
time: 211 us
  blocking collectives  123 us (58%)
  waiting for transfers between devices  55.3 us (26%)
  matrix products  14.4 us (7%)
  between operations  14.1 us (7%)
  other arithmetic  2.61 us (1%)
    all_gather x1, blocking collectives, per_device(): lax.all_gather(phi_param, 'seq', axis=0, tiled=True)  31.8 us
    all_gather x1, blocking collectives, per_device(): lax.all_gather(slot_grad[0], 'seq', axis=0, tiled=True)  31.5 us
    psum x1, waiting for transfers between devices, per_device(): phi_grad = lax.psum(phi_share, 'batch')  28.3 us
    reduce_scatter x1, waiting for transfers between devices, per_device(): lax.psum_scatter(phi_terms, 'seq', scatter_dimension=0, tiled=True)  26.9 us
    pmax x1, blocking collectives, per_device(): col_peak = lax.pmax(jnp.max(scores, axis=0, keepdims=True), 'seq')  23.2 us
    psum x1, blocking collectives, per_device(): lax.psum(jnp.sum(dispatch * weight_grad, axis=0, keepdims=True), 'seq')  19.4 us
    psum x1, blocking collectives, per_device(): col_total = lax.psum(jnp.sum(raw_weights, axis=0, keepdims=True), 'seq')  17.1 us
    dot_general x1, matrix products, per_device(): lax.dot_general(logit_grad, phi_full, (((1,), (1,)), ((), ())), preferred...  4.68 us
  transfers between devices with their start and end apart: 2, of which 2 were waited for; matrix products, arithmetic and copies ran while one was open for 4% of the time, Pallas kernels for 0%

commit v1 on v0

--- a/solution.py
+++ b/solution.py
@@ -31,7 +31,7 @@
         inputs, logit_grad, (((0,), (0,)), ((), ())), preferred_element_type=jnp.float32
     )
     phi_share = lax.psum_scatter(phi_terms, "seq", scatter_dimension=0, tiled=True)
-    phi_grad = lax.psum(phi_share, "batch")
+    phi_grad = jnp.sum(lax.all_gather(phi_share, "batch"), 0)
     return (token_grad, phi_grad)
 
 

time: 211 us -> 185 us (0.88)
  waiting for transfers between devices: 55.3 us -> 27.1 us
  blocking collectives: 123 us -> 130 us
  matrix products: 14.4 us -> 8.78 us
    psum x1 -> x0, waiting for transfers between devices: 28.3 us -> none  [per_device(): phi_grad = lax.psum(phi_share, 'batch')]
    all_gather x0 -> x1, blocking collectives: none -> 7.36 us  [per_device(): phi_grad = jnp.sum(lax.all_gather(phi_share, 'batch'), 0)]
    dot_general x1, matrix products: 3.68 us -> 0.71 us  [per_device(): jnp.dot(dispatch_low, upstream, preferred_element_type=jnp.float32)]
    dot_general x1, matrix products: 4.68 us -> 2.19 us  [per_device(): lax.dot_general(logit_grad, phi_full, (((1,), (1,)), ((), ())), preferred...]
  transfers between devices with their start and end apart: 2 -> 1, of which waited for: 2 -> 1; matrix products, arithmetic and copies ran while one was open for 4% -> 2% of each run, Pallas kernels for 0% -> 0%
where the time goes in v1:
time: 185 us
  blocking collectives  130 us (70%)
  waiting for transfers between devices  27.1 us (15%)
  between operations  14.1 us (8%)
  matrix products  8.78 us (5%)
  other arithmetic  2.91 us (2%)
    all_gather x1, blocking collectives, per_device(): lax.all_gather(phi_param, 'seq', axis=0, tiled=True)  31.8 us
    all_gather x1, blocking collectives, per_device(): lax.all_gather(slot_grad[0], 'seq', axis=0, tiled=True)  31.4 us
    reduce_scatter x1, waiting for transfers between devices, per_device(): lax.psum_scatter(phi_terms, 'seq', scatter_dimension=0, tiled=True)  27.1 us
    pmax x1, blocking collectives, per_device(): col_peak = lax.pmax(jnp.max(scores, axis=0, keepdims=True), 'seq')  23.2 us
    psum x1, blocking collectives, per_device(): lax.psum(jnp.sum(dispatch * weight_grad, axis=0, keepdims=True), 'seq')  19.4 us
    psum x1, blocking collectives, per_device(): col_total = lax.psum(jnp.sum(raw_weights, axis=0, keepdims=True), 'seq')  17.1 us
    all_gather x1, blocking collectives, per_device(): phi_grad = jnp.sum(lax.all_gather(phi_share, 'batch'), 0)  7.36 us
  transfers between devices with their start and end apart: 1, of which 1 were waited for; matrix products, arithmetic and copies ran while one was open for 2% of the time, Pallas kernels for 0%

profile of v1, /device:TPU:0, one launch (start us, length us, event | category | flops | bytes accessed | tf_op | source)
XLA Modules:
  0.0 184.6 jit_solution(1900664875650321618)
XLA Ops:
  7.2 0.0 copy-start
  7.2 0.0 reduce-scatter.2.cloned.1.call-start
  7.2 1.3 reduce_max.16
  8.6 23.2 %pmax.7 = f32[256]{0:T(256)S(1)} all-reduce(bf16[256]{0:T(256)(128)(2,1)S(1)} %reduce_max.16), channel_id=1, replica_groups=mesh['seq'=8,'batch'=4] {'seq'}, use_global_device_ids=true, to_apply=%region_1.0 | all-reduce | flops 256 | bytes 1536 | tf_op jit(solution)/shard_map/pmax | solution.py:17
  31.7 1.3 fusion.10
  33.0 17.1 %psum.14 = f32[256]{0:T(256)S(1)} all-reduce(f32[256]{0:T(256)S(1)} %fusion.10), channel_id=1, replica_groups=mesh['seq'=8,'batch'=4] {'seq'}, use_global_device_ids=true, to_apply=%region_3.0 | all-reduce | flops 256 | bytes 2048 | tf_op jit(solution)/shard_map/psum | solution.py:19
  50.1 31.4 %all-gather = bf16[1,256,1024]{2,1,0:T(8,128)(2,1)S(1)} all-gather(bf16[1,32,1024]{2,1,0:T(8,128)(2,1)} %param.6), channel_id=2, replica_groups=mesh['seq'=8,'batch'=4] {'seq'}, dimensions={1}, use_global_device_ids=true | all-gather | bytes 589824 | tf_op jit(solution)/shard_map/all_gather | solution.py:11
  81.5 0.0 copy-done
  81.5 0.0 copy-start.1
  81.5 2.8 %multiply_reduce_fusion = (f32[256]{0:T(256)S(1)}, f32[1024,256]{1,0:T(8,128)}) fusion(f32[256]{0:T(256)S(1)} %psum.14, f32[256]{0:T(256)S(1)} %pmax.7, bf16[1,1024,256]{2,1,0:T(8,128)(2,1)} %param.5, bf16[1,256,1024]{2,1,0:T(8,128)(2,1)S(1)} %all-gather, bf16[1,1024,1024]{2,1,0:T(8,128)(2,1)S(1)} %copy-done), kind=kOutput, calls=%fused_computation.12 | convolution fusion | flops 538181376 | bytes 4197376 | tf_op jit(solution)/shard_map/dot_general | solution.py:14
  84.4 19.4 %psum.15 = f32[256]{0:T(256)S(1)} all-reduce(f32[256]{0:T(256)S(1)} %get-tuple-element.4), channel_id=1, replica_groups=mesh['seq'=8,'batch'=4] {'seq'}, use_global_device_ids=true, to_apply=%region_5.0 | all-reduce | flops 256 | bytes 2048 | tf_op jit(solution)/shard_map/psum | solution.py:21
  103.7 0.0 copy-done.1
  103.7 0.0 copy-start.3
  103.7 3.0 %fusion.5 = f32[1024,256]{0,1:T(8,128)} fusion(bf16[1,1024,1024]{2,1,0:T(8,128)(2,1)S(1)} %copy-done, f32[1024,256]{1,0:T(8,128)} %get-tuple-element.5, f32[256]{0:T(256)S(1)} %psum.15, f32[256]{0:T(256)S(1)} %psum.14, f32[256]{0:T(256)S(1)} %pmax.7, bf16[1,1024,256]{2,1,0:T(8,128)(2,1)S(1)} %copy-done.1), kind=kOutput, calls=%fused_computation.6 | convolution fusion | flops 538443776 | bytes 4721664 | tf_op jit(solution)/shard_map/dot_general | solution.py:30
  106.8 0.0 reduce-scatter.2.cloned.1.call-update
  106.8 0.0 copy-done.3
  106.8 31.8 %all_gather.13 = bf16[1024,256]{1,0:T(8,128)(2,1)S(1)} all-gather(bf16[128,256]{1,0:T(8,128)(2,1)S(1)} %copy-done.3), channel_id=1, replica_groups=mesh['seq'=8,'batch'=4] {'seq'}, dimensions={0}, use_global_device_ids=true | all-gather | bytes 589824 | tf_op jit(solution)/shard_map/all_gather | solution.py:12
  138.7 0.0 copy-start.2
  138.7 0.7 fusion.12
  139.4 0.5 copy-done.2
  139.9 2.2 %fusion.4 = bf16[1,1024,1024]{2,1,0:T(8,128)(2,1)} fusion(f32[1024,1024]{1,0:T(8,128)S(1)} %fusion.12, bf16[1024,256]{1,0:T(8,128)(2,1)S(1)} %all_gather.13, f32[1024,256]{1,0:T(8,128)S(1)} %copy-done.2, f32[256]{0:T(256)S(1)} %psum.15, f32[256]{0:T(256)S(1)} %psum.14, f32[256]{0:T(256)S(1)} %pmax.7, bf16[1,1024,256]{2,1,0:T(8,128)(2,1)S(1)} %copy-done.1), kind=kOutput, calls=%fused_computation.5 | convolution fusion | flops 541589504 | bytes 8391680 | tf_op jit(solution)/shard_map/dot_general | solution.py:26
  142.1 27.1 %reduce-scatter.2.cloned.1.call-done = f32[128,256]{0,1:T(8,128)} async-done(((f32[1024,256]{0,1:T(8,128)}), f32[128,256]{0,1:T(8,128)}) %reduce-scatter.2.cloned.1.call-update) | async-done | bytes 131088 | tf_op jit(solution)/shard_map/reduce_scatter | solution.py:33
  169.1 7.4 %all-gather.1 = f32[512,256]{0,1:T(8,128)S(1)} all-gather(f32[128,256]{0,1:T(8,128)} %reduce-scatter.2.cloned.1.call-done), channel_id=3, replica_groups=mesh['seq'=8,'batch'=4] {'batch'}, dimensions={0}, use_global_device_ids=true | all-gather | bytes 655360 | tf_op jit(solution)/shard_map/all_gather | solution.py:34
  176.5 0.2 reshape.21
  176.7 0.3 reduce_sum.29
  177.0 0.8 copy.6
Async XLA Ops:
  7.2 74.4 %copy-start = (bf16[1,1024,1024]{2,1,0:T(8,128)(2,1)S(1)}, bf16[1,1024,1024]{2,1,0:T(8,128)(2,1)}, u32[]{:S(2)}) copy-start(bf16[1,1024,1024]{2,1,0:T(8,128)(2,1)} %param.4) | copy-start | bytes 6291460
  7.2 162.0 %reduce-scatter.2.cloned.1.call-start = ((), (), s32[]{:S(2)}) async-start(), calls=%async_computation.1 | async-start | bytes 1179648 | tf_op jit(solution)/shard_map/reduce_scatter | solution.py:33
  81.5 22.2 %copy-start.1 = (bf16[1,1024,256]{2,1,0:T(8,128)(2,1)S(1)}, bf16[1,1024,256]{2,1,0:T(8,128)(2,1)}, u32[]{:S(2)}) copy-start(bf16[1,1024,256]{2,1,0:T(8,128)(2,1)} %param.5) | copy-start | bytes 1572868
  103.7 3.1 %copy-start.3 = (bf16[128,256]{1,0:T(8,128)(2,1)S(1)}, bf16[128,256]{1,0:T(8,128)(2,1)}, u32[]{:S(2)}) copy-start(bf16[128,256]{1,0:T(8,128)(2,1)} %param.7) | copy-start | bytes 196612
  138.7 1.2 copy-start.2
Sparse Core Ops, SparseCore 0:
  106.9 62.1 reduce-scatter.1
